TPU v7x, 32 devices: a whole 2x2x4 slice. The times are simulated.
32 devices in a mesh: replica: 4 (over z), tp: 8 (over y, x, core).
Axes of the slice: x: 2, y: 2, z: 4, core: 2. Of those that a mesh axis runs over, the one named last changes fastest.
Arguments:
- hidden: bfloat16 [256, 8192], P(('replica', 'tp')), may hold values from -64 to 64
- head: bfloat16 [152064, 8192], P(('replica', 'tp'))
- token_ids: int32 [256], replicated, may hold values from 0 to 152063
Outputs:
- logprob: float32 [256], P(('replica', 'tp'))
All inputs are finite; a program needn't handle non-finite values.
Results may differ from a plain program's by a relative error of at most 0.0003.
Values may be sent and summed in bfloat16 or wider, within the bound.
A program may use at most 128 MiB of HBM per device.

v0:
```python
import functools

import jax
import jax.numpy as jnp
from jax import lax
from jax.experimental import pallas as pl
from jax.experimental.pallas import tpu as pltpu
from jax.sharding import PartitionSpec as P

MESH = pl.DeviceIdType.MESH
SLICES = 4
PIECES = 2 * SLICES
VMEM = 66_000_000


def chunk_rows(rows, limit):
    return max((r for r in range(8, limit + 1, 8) if rows % r == 0), default=rows)


def split_axis(size):
    return (size // 4, 2, 2) if size % 4 == 0 else (size, 1, 1)


def kernel(dims, rows, slots, tokens_ref, hidden_ref, head_ref, out_ref, ring, acc, gathered, hid,
           stats, sent, arrived, ring_sem, own_sem, gsend, grecv, ssend, srecv):
    z_n, y_n, x_n, c_n = dims
    tp_n = y_n * x_n * c_n
    devices = z_n * tp_n
    z = lax.axis_index("replica")
    t = lax.axis_index("tp")
    me = z * tp_n + t
    y, x, c = t // (x_n * c_n), (t // c_n) % x_n, t % c_n
    at = (z, y, x, c)
    per_device, depth = hidden_ref.shape
    local_vocab = head_ref.shape[0]
    seqs = hid.shape[0]
    piece_k, slice_k = depth // PIECES, depth // SLICES
    chunks = local_vocab // rows
    blocks = chunks * SLICES

    def fetch(i, slot):
        s, k = i // chunks, i % chunks
        return pltpu.make_async_copy(
            head_ref.at[pl.ds(pl.multiple_of(k * rows, 8), rows), pl.ds(pl.multiple_of(s * slice_k, 128), slice_k)],
            ring.at[slot], ring_sem.at[slot])

    def own(p):
        return pltpu.make_async_copy(
            hidden_ref.at[:, pl.ds(p * piece_k, piece_k)], gathered.at[p, z, y, x, c], own_sem.at[p])

    for p in range(PIECES):
        own(p).start()

    @pl.loop(0, slots)
    def _(i):
        fetch(i, i).start()

    barrier = pltpu.get_barrier_semaphore()

    @pl.loop(1, devices)
    def _(k):
        d = (me + k) % devices
        pl.semaphore_signal(barrier, inc=1, device_id=(d // tp_n, d % tp_n), device_id_type=MESH)

    pl.semaphore_wait(barrier, devices - 1)

    def order(p):
        return (0, 1, 2, 3) if p % 2 == 0 else (0, 2, 1, 3)

    def copy(p, phase, k, incoming=False):
        path = order(p)
        axis = path[phase]
        n = dims[axis]
        there = list(at)
        there[axis] = (at[axis] + k) % n
        mine = at[axis] if not incoming else (at[axis] + n - k) % n
        index = [p]
        for a in range(4):
            if a in path[:phase]:
                index.append(slice(None))
            elif a == axis:
                index.append(mine)
            else:
                index.append(at[a])
        ref = gathered.at[tuple(index)]
        device = (there[0], (there[1] * x_n + there[2]) * c_n + there[3])
        return pltpu.make_async_remote_copy(
            src_ref=ref, dst_ref=ref, send_sem=gsend.at[p, phase, k - 1], recv_sem=grecv.at[p, phase, k - 1],
            device_id=device, device_id_type=MESH)

    def hops(p, phase):
        return range(1, dims[order(p)[phase]])

    def arrive(p, phase):
        for k in hops(p, phase):
            copy(p, phase, k, incoming=True).wait_recv()

    def step(s, phase):
        for p in (2 * s, 2 * s + 1):
            if phase == 0:
                own(p).wait()
            else:
                arrive(p, phase - 1)
            for k in hops(p, phase):
                copy(p, phase, k).start()

    def finish(s):
        for p in (2 * s, 2 * s + 1):
            arrive(p, 3)
            block = gathered[p].astype(jnp.float32).reshape(seqs, piece_k)
            hid[:, p * piece_k:(p + 1) * piece_k] = block.astype(jnp.bfloat16)

    stats[0:1, :] = jnp.full((1, seqs), -jnp.inf, jnp.float32)
    stats[1:3, :] = jnp.zeros((2, seqs), jnp.float32)

    def compute(s, low, high):
        def body(k, carry):
            i = s * chunks + k
            slot = i % slots
            fetch(i, slot).wait()
            part = lax.dot_general(ring[slot], hid[:, s * slice_k:(s + 1) * slice_k], (((1,), (1,)), ((), ())),
                                   preferred_element_type=jnp.float32)
            place = pl.ds(pl.multiple_of(k * rows, 8), rows)
            if s == 0:
                acc[place, :] = part
            elif s < SLICES - 1:
                acc[place, :] += part
            else:
                logits = acc[place, :] + part
                top = stats[0:1, :]
                new_top = jnp.maximum(top, jnp.max(logits, axis=0, keepdims=True))
                column = lax.broadcasted_iota(jnp.int32, logits.shape, 0) + (me * local_vocab + k * rows)
                hit = jnp.where(column == tokens_ref[...], logits, 0.0)
                total = jnp.sum(jnp.exp(logits - new_top), axis=0, keepdims=True)
                stats[0:1, :] = new_top
                stats[1:2, :] = stats[1:2, :] * jnp.exp(top - new_top) + total
                stats[2:3, :] += jnp.sum(hit, axis=0, keepdims=True)

            @pl.when(i + slots < blocks)
            def _():
                fetch(i + slots, slot).start()
            return carry
        lax.fori_loop(low, high, body, 0)

    for s in range(SLICES):
        step(s, 0)
    todo = [(s, w - s + 1) for w in range(3 + SLICES) for s in range(SLICES) if 1 <= w - s + 1 <= 3]
    first = todo.index((0, 3)) + 1
    for s, phase in todo[:first]:
        step(s, phase)
    rest = todo[first:]
    parts = max(1, min(chunks, len(rest)))
    edges = [chunks * j // parts for j in range(parts + 1)]
    finish(0)
    for j in range(parts):
        for s, phase in rest[len(rest) * j // parts:len(rest) * (j + 1) // parts]:
            step(s, phase)
        compute(0, edges[j], edges[j + 1])
    for s in range(1, SLICES):
        finish(s)
        compute(s, 0, chunks)

    line = lax.broadcasted_iota(jnp.int32, (128, seqs), 0)
    table = jnp.where(line == 0, stats[0:1, :], jnp.where(line == 1, stats[1:2, :], stats[2:3, :]))
    sent[...] = table.T.reshape(devices, per_device, 128)
    arrived[pl.ds(me, 1)] = sent[pl.ds(me, 1)]

    def result(k, incoming=False):
        d = (me + k) % devices
        origin = (me + devices - k) % devices if incoming else me
        return pltpu.make_async_remote_copy(
            src_ref=sent.at[d], dst_ref=arrived.at[origin], send_sem=ssend.at[k], recv_sem=srecv.at[k],
            device_id=(d // tp_n, d % tp_n), device_id_type=MESH)

    @pl.loop(1, devices)
    def _(k):
        result(k).start()

    for p in range(PIECES):
        for phase in range(4):
            for k in hops(p, phase):
                copy(p, phase, k).wait_send()

    @pl.loop(1, devices)
    def _(k):
        result(k, incoming=True).wait_recv()
        result(k).wait_send()

    table = arrived[...]
    tops, totals, picked = table[:, :, 0:1], table[:, :, 1:2], table[:, :, 2:3]
    top = jnp.max(tops, axis=0)
    total = jnp.sum(totals * jnp.exp(tops - top[None]), axis=0)
    value = jnp.sum(picked, axis=0) - top - jnp.log(total)
    out_ref[...] = jnp.broadcast_to(value, out_ref.shape)


def shards(z_n, tp_n, hidden, head, token_ids):
    dims = (z_n,) + split_axis(tp_n)
    devices = z_n * tp_n
    per_device, depth = hidden.shape
    seqs = per_device * devices
    rows = chunk_rows(head.shape[0], 528)
    blocks = head.shape[0] // rows * SLICES
    block_bytes = rows * depth // SLICES * 2
    fixed = head.shape[0] * seqs * 4 + 2 * seqs * depth * 2 + 2 * rows * seqs * 4 + 3 * 2**20
    slots = max(2, min(blocks, (VMEM - fixed) // block_bytes))
    hop_n = max(max(dims) - 1, 1)
    out = pl.pallas_call(
        functools.partial(kernel, dims, rows, slots),
        out_shape=jax.ShapeDtypeStruct((per_device, 128), jnp.float32),
        in_specs=[pl.BlockSpec(memory_space=pltpu.VMEM), pl.BlockSpec(memory_space=pltpu.HBM),
                  pl.BlockSpec(memory_space=pltpu.HBM)],
        out_specs=pl.BlockSpec(memory_space=pltpu.VMEM),
        scratch_shapes=[
            pltpu.VMEM((slots, rows, depth // SLICES), jnp.bfloat16),
            pltpu.VMEM((head.shape[0], seqs), jnp.float32),
            pltpu.VMEM((PIECES,) + dims + (per_device, depth // PIECES), jnp.bfloat16),
            pltpu.VMEM((seqs, depth), jnp.bfloat16),
            pltpu.VMEM((8, seqs), jnp.float32),
            pltpu.VMEM((devices, per_device, 128), jnp.float32),
            pltpu.VMEM((devices, per_device, 128), jnp.float32),
            pltpu.SemaphoreType.DMA((slots,)),
            pltpu.SemaphoreType.DMA((PIECES,)),
            pltpu.SemaphoreType.DMA((PIECES, 4, hop_n)),
            pltpu.SemaphoreType.DMA((PIECES, 4, hop_n)),
            pltpu.SemaphoreType.DMA((devices,)),
            pltpu.SemaphoreType.DMA((devices,)),
        ],
        compiler_params=pltpu.CompilerParams(
            collective_id=0, has_side_effects=True, vmem_limit_bytes=67_000_000),
    )(token_ids.reshape(1, seqs), hidden, head)
    return out[:, 0]


def solution(mesh):
    in_specs = (P(("replica", "tp"), None), P(("replica", "tp"), None), P())
    body = functools.partial(shards, mesh.shape["replica"], mesh.shape["tp"])
    return jax.shard_map(body, mesh=mesh, in_specs=in_specs, out_specs=P(("replica", "tp")), check_vma=False)
```

profile of v0, /device:TPU:0, one launch (start us, length us, event | category | flops | bytes accessed | tf_op | source)
XLA Modules:
  0.0 72.5 jit_solution(17236863449492968058)
XLA Ops:
  0.0 71.2 %shard_map.37 = f32[8,128]{1,0:T(8,128)} custom-call(s32[1,256]{1,0:T(1,128)} %bitcast.1, bf16[8,8192]{1,0:T(8,128)(2,1)} %hidden_ref.1, bf16[4752,8192]{1,0:T(8,128)(2,1)} %head_ref.1), custom_call_target="tpu_custom_call" | custom-call | tf_op jit(solution)/shard_map/pallas_call | solution.py:208
  71.2 1.3 %slice_reduce_fusion = f32[8]{0:T(128)} fusion(f32[8,128]{1,0:T(8,128)} %shard_map.37), kind=kLoop, calls=%fused_computation | loop fusion | bytes 64 | tf_op jit(solution)/shard_map/slice | solution.py:232
where the time goes:
time: 72.7 us; the launch traced here: 72.5 us
  Pallas kernels  71.2 us (98%)
  local copies, waits for them, and re-layouts  1.31 us (2%)
    pallas_call x1, Pallas kernels, shards(): pl.pallas_call(functools.partial(kernel, dims, rows, slots), out_shape=ja...  71.2 us

commit v1 on v0

v1 whole, which is shorter than its diff:
```python
import functools

import jax
import jax.numpy as jnp
from jax import lax
from jax.experimental import pallas as pl
from jax.experimental.pallas import tpu as pltpu
from jax.sharding import PartitionSpec as P

MESH = pl.DeviceIdType.MESH
VMEM = 66_500_000
UNITS = 16
SINGLES = 4
PAIR = 2
LEAD = (4, 2)
COMM = True
COMPUTE = True


def chunk_rows(rows, limit):
    return max((r for r in range(16, limit + 1, 16) if rows % r == 0), default=rows)


def split_axis(size):
    return (size // 4, 2, 2) if size % 4 == 0 else (size, 1, 1)


def kernel(dims, unit, rows, tokens_ref, hidden_ref, head_ref, out_ref, ring, acc, gathered_a, gathered_b, hid,
           sent, arrived, ring_sem, own_sem, gsend, grecv, ssend, srecv):
    z_n, y_n, x_n, c_n = dims
    tp_n = y_n * x_n * c_n
    devices = z_n * tp_n
    z = lax.axis_index("replica")
    t = lax.axis_index("tp")
    me = z * tp_n + t
    y, x, c = t // (x_n * c_n), (t // c_n) % x_n, t % c_n
    at = (z, y, x, c)
    per_device, depth = hidden_ref.shape
    local_vocab = head_ref.shape[0]
    seqs = hid.shape[0]
    slots = ring.shape[0]
    gathered = (gathered_a, gathered_b)
    half = unit // 2

    def order(h):
        return (0, 1, 2, 3) if h % 2 == 0 else (0, 2, 1, 3)

    def columns(u, width=unit):
        return pl.ds(pl.multiple_of(u * unit, 128), width)

    def fetch(i):
        slot = i % slots
        return pltpu.make_async_copy(head_ref.at[:, columns(i * PAIR, PAIR * unit)], ring.at[slot], ring_sem.at[slot])

    def own(u, h):
        there = tuple(at[a] for a in reversed(order(h)))
        return pltpu.make_async_copy(
            hidden_ref.at[:, pl.ds(pl.multiple_of(u * unit + h * half, 128), half)],
            gathered[h].at[(u,) + there], own_sem.at[h])

    @pl.loop(0, UNITS)
    def _(u):
        own(u, 0).start()
        own(u, 1).start()

    @pl.loop(0, slots)
    def _(i):
        fetch(i).start()

    acc[...] = jnp.zeros_like(acc)

    def device(there):
        return (there[0], (there[1] * x_n + there[2]) * c_n + there[3])

    def peer(axis, k):
        there = list(at)
        there[axis] = (at[axis] + k) % dims[axis]
        return device(there)

    if COMM:
        barrier = pltpu.get_barrier_semaphore()
        for axis in range(4):
            for k in range(1, dims[axis]):
                pl.semaphore_signal(barrier, inc=1, device_id=peer(axis, k), device_id_type=MESH)
        pl.semaphore_wait(barrier, sum(dims) - 4)

    def remote(ref, h, phase, u, where):
        return pltpu.make_async_remote_copy(
            src_ref=ref, dst_ref=ref, send_sem=gsend.at[h, phase], recv_sem=grecv.at[u, h, phase],
            device_id=where, device_id_type=MESH)

    def block(u, h, phase):
        path = order(h)
        index = [slice(None) if a in path[:phase] else at[a] for a in reversed(path)]
        return gathered[h].at[(u,) + tuple(index)]

    def some(u, h, phase):
        count = dims[order(h)[phase]] - 1
        return gathered[h].at[(u,) + (0,) * (3 - phase) + (pl.ds(0, count),)]

    def hops(h, phase):
        return range(1, dims[order(h)[phase]])

    def arrive(u, h, phase):
        if dims[order(h)[phase]] > 1:
            remote(some(u, h, phase), h, phase, u, peer(3, 0)).wait_recv()

    def step(u, phase):
        if not COMM:
            return
        for h in (0, 1):
            if phase > 0:
                arrive(u, h, phase - 1)
            for k in hops(h, phase):
                remote(block(u, h, phase), h, phase, u, peer(order(h)[phase], k)).start()

    def finish(u):
        if COMM:
            for h in (0, 1):
                arrive(u, h, 3)
        for h in (0, 1):
            part = pl.ds(pl.multiple_of(u * unit + h * half, 128), half)
            for d in range(0, devices, 2):
                block = []
                for e in (d, d + 1):
                    there = (e // tp_n, e // (x_n * c_n) % y_n, e // c_n % x_n, e % c_n)
                    block.append(gathered[h][(u,) + tuple(there[a] for a in reversed(order(h)))].astype(jnp.float32))
                hid[d * per_device:(d + 2) * per_device, part] = jnp.concatenate(block, 0).astype(jnp.bfloat16)

    def product(u, low, count, width):
        spot = pl.ds(pl.multiple_of(u % PAIR * unit, 128), width)
        return lax.dot_general(ring[u // PAIR % slots, pl.ds(low, count), spot], hid[:, columns(u, width)],
                               (((1,), (1,)), ((), ())), preferred_element_type=jnp.float32)

    for h in (0, 1):
        there = tuple(at[a] for a in reversed(order(h)))
        mine = gathered[h].at[(slice(None),) + there]
        pltpu.make_async_copy(mine, mine, own_sem.at[h]).wait()

    @pl.loop(0, UNITS)
    def _(u):
        step(u, 0)

    first = [(u, 3) for u in range(2)] + [(u, 2) for u in range(2 + LEAD[1])] + [(u, 1) for u in range(2 + LEAD[0])]
    for u, phase in sorted(first, key=lambda e: (e[0] + 2 * e[1], e[1])):
        step(u, phase)

    def advance(u):
        for phase, lead in ((3, 0), (2, LEAD[1]), (1, LEAD[0])):
            @pl.when(u + lead < UNITS)
            def _():
                step(u + lead, phase)

    def ready(u, count):
        for v in range(count):
            finish(u + v)

        @pl.when(u % PAIR == 0)
        def _():
            fetch(u // PAIR).wait()

    def compute(u, count):
        ready(u, count)
        if COMPUTE:
            acc[...] += product(u, 0, local_vocab, count * unit)

        @pl.when(((u + count) % PAIR == 0) & (u // PAIR + slots < UNITS // PAIR))
        def _():
            fetch(u // PAIR + slots).start()

    @pl.loop(0, SINGLES)
    def _(u):
        @pl.when(u > 0)
        def _():
            advance(u + 1 + u // (SINGLES - 1))

        @pl.when(u == SINGLES - 2)
        def _():
            advance(u + 2)
        compute(u, 1)

    pairs = (UNITS - SINGLES) // PAIR - 1

    @pl.loop(0, pairs)
    def _(i):
        for v in range(PAIR):
            advance(SINGLES + (i + 1) * PAIR + v)
        compute(SINGLES + i * PAIR, PAIR)

    final = UNITS - PAIR
    ready(final, PAIR)
    tokens = tokens_ref[...] - me * local_vocab
    blocks = local_vocab // rows
    inner = 3 if blocks % 3 == 0 else 1

    big = rows * inner

    def measure(i, carry):
        top, total, picked = carry
        for b in range(inner):
            low = pl.multiple_of(i * big + b * rows, 8)
            logits = acc[pl.ds(low, rows), :]
            new_top = jnp.maximum(top, jnp.max(logits, axis=0, keepdims=True))
            line = lax.broadcasted_iota(jnp.int32, logits.shape, 0)
            picked += jnp.sum(jnp.where(line == tokens - low, logits, 0.0), axis=0, keepdims=True)
            total = total * jnp.exp(top - new_top) + jnp.sum(jnp.exp(logits - new_top), axis=0, keepdims=True)
            top = new_top
        return top, total, picked

    def finalize(i):
        low = pl.multiple_of(i * big, 8)
        acc[pl.ds(low, big), :] += product(final, low, big, PAIR * unit)

    def close(i, carry):
        carry = measure(i - 1, carry)
        finalize(i)
        return carry

    carry = (jnp.full((1, seqs), -jnp.inf, jnp.float32),) + (jnp.zeros((1, seqs), jnp.float32),) * 2
    finalize(0)
    carry = lax.fori_loop(1, blocks // inner, close, carry)
    top, total, picked = measure(blocks // inner - 1, carry)

    groups, _, _, lanes = sent.shape
    for g in range(groups):
        part = slice(g * lanes, (g + 1) * lanes)
        sent[g, 0, 0:1, :] = top[:, part]
        sent[g, 0, 1:2, :] = picked[:, part]
        sent[g, 1, :, :] = jnp.broadcast_to(total[:, part], (2, lanes))
    apart = lanes // per_device

    if COMM:
        arrived[pl.ds(me, 1)] = sent[pl.ds(me // apart, 1)]

    def result(k):
        d = (me + k) % devices
        return pltpu.make_async_remote_copy(
            src_ref=sent.at[d // apart], dst_ref=arrived.at[me], send_sem=ssend, recv_sem=srecv,
            device_id=(d // tp_n, d % tp_n), device_id_type=MESH)

    if COMM:
        @pl.loop(1, devices)
        def _(k):
            result(k).start()

        for h in (0, 1):
            for phase in range(4):
                if dims[order(h)[phase]] > 1:
                    remote(some(slice(None), h, phase), h, phase, 0, peer(3, 0)).wait_send()

        if devices > 1:
            everyone = pltpu.make_async_remote_copy(
                src_ref=arrived.at[pl.ds(0, devices - 1)], dst_ref=arrived.at[pl.ds(0, devices - 1)],
                send_sem=ssend, recv_sem=srecv, device_id=peer(3, 0), device_id_type=MESH)
            everyone.wait_recv()
            everyone.wait_send()

    firsts, totals = arrived[:, 0], arrived[:, 1]
    top = jnp.max(firsts, axis=0)
    total = jnp.sum(totals * jnp.exp(firsts - top), axis=0)
    picked = jnp.sum(firsts, axis=0)
    value = picked[1:2] - top[0:1] - jnp.log(total[0:1])
    lane = lax.broadcasted_iota(jnp.int32, (per_device, lanes), 1)
    row = lax.broadcasted_iota(jnp.int32, (per_device, lanes), 0) + (me % apart) * per_device
    mine = jnp.sum(jnp.where(lane == row, value, 0.0), axis=1, keepdims=True)
    out_ref[...] = jnp.broadcast_to(mine, out_ref.shape)


def shards(z_n, tp_n, hidden, head, token_ids):
    dims = (z_n,) + split_axis(tp_n)
    devices = z_n * tp_n
    per_device, depth = hidden.shape
    local_vocab = head.shape[0]
    seqs = per_device * devices
    rows = chunk_rows(local_vocab, 528)
    unit = depth // UNITS
    fixed = local_vocab * seqs * 4 + 2 * seqs * depth * 2 + 3 * 2**20
    wide = PAIR * unit
    slots = min(depth // wide, (VMEM - fixed - local_vocab * seqs * 5) // (local_vocab * wide * 2))
    stores = [tuple(dims[a] for a in reversed(path)) for path in ((0, 1, 2, 3), (0, 2, 1, 3))]
    lanes = 128
    out = pl.pallas_call(
        functools.partial(kernel, dims, unit, rows),
        out_shape=jax.ShapeDtypeStruct((per_device, 128), jnp.float32),
        in_specs=[pl.BlockSpec(memory_space=pltpu.VMEM), pl.BlockSpec(memory_space=pltpu.HBM),
                  pl.BlockSpec(memory_space=pltpu.HBM)],
        out_specs=pl.BlockSpec(memory_space=pltpu.VMEM),
        scratch_shapes=[
            pltpu.VMEM((slots, local_vocab, wide), jnp.bfloat16),
            pltpu.VMEM((local_vocab, seqs), jnp.float32),
            pltpu.VMEM((UNITS,) + stores[0] + (per_device, unit // 2), jnp.bfloat16),
            pltpu.VMEM((UNITS,) + stores[1] + (per_device, unit // 2), jnp.bfloat16),
            pltpu.VMEM((seqs, depth), jnp.bfloat16),
            pltpu.VMEM((seqs // lanes, 2, 2, lanes), jnp.float32),
            pltpu.VMEM((devices, 2, 2, lanes), jnp.float32),
            pltpu.SemaphoreType.DMA((slots,)),
            pltpu.SemaphoreType.DMA((2,)),
            pltpu.SemaphoreType.DMA((2, 4)),
            pltpu.SemaphoreType.DMA((UNITS, 2, 4)),
            pltpu.SemaphoreType.DMA,
            pltpu.SemaphoreType.DMA,
        ],
        compiler_params=pltpu.CompilerParams(
            has_side_effects=True, vmem_limit_bytes=67_000_000, **(dict(collective_id=0) if COMM else {})),
    )(token_ids.reshape(1, seqs), hidden, head)
    return out[:, 0]


def solution(mesh):
    in_specs = (P(("replica", "tp"), None), P(("replica", "tp"), None), P())
    body = functools.partial(shards, mesh.shape["replica"], mesh.shape["tp"])
    return jax.shard_map(body, mesh=mesh, in_specs=in_specs, out_specs=P(("replica", "tp")), check_vma=False)
```

time: 72.7 us -> 56 us (0.77)
  Pallas kernels: 71.2 us -> 54.4 us
    pallas_call x1, Pallas kernels: 71.2 us -> 54.4 us  [shards(): pl.pallas_call(functools.partial(kernel, dims, unit, rows), out_shape=jax...]
where the time goes in v1:
time: 56 us; the launch traced here: 55.8 us
  Pallas kernels  54.4 us (97%)
  local copies, waits for them, and re-layouts  1.31 us (2%)
    pallas_call x1, Pallas kernels, shards(): pl.pallas_call(functools.partial(kernel, dims, unit, rows), out_shape=jax...  54.4 us
    slice x1, local copies, waits for them, and re-layouts, shards(): return out[:, 0]  1.31 us

profile of v1, /device:TPU:0, one launch (start us, length us, event | category | flops | bytes accessed | tf_op | source)
XLA Modules:
  0.0 55.8 jit_solution(2269966422941139215)
XLA Ops:
  0.0 54.4 %shard_map.37 = f32[8,128]{1,0:T(8,128)} custom-call(s32[1,256]{1,0:T(1,128)} %bitcast.1, bf16[8,8192]{1,0:T(8,128)(2,1)} %hidden_ref.1, bf16[4752,8192]{1,0:T(8,128)(2,1)} %head_ref.1), custom_call_target="tpu_custom_call" | custom-call | tf_op jit(solution)/shard_map/pallas_call | solution.py:282
  54.5 1.3 %slice_reduce_fusion = f32[8]{0:T(128)} fusion(f32[8,128]{1,0:T(8,128)} %shard_map.37), kind=kLoop, calls=%fused_computation | loop fusion | bytes 64 | tf_op jit(solution)/shard_map/slice | solution.py:306

commit v2 on v1

--- a/solution.py
+++ b/solution.py
@@ -12,7 +12,7 @@
 UNITS = 16
 SINGLES = 4
 PAIR = 2
-LEAD = (4, 2)
+LEAD = (5, 2)
 COMM = True
 COMPUTE = True
 
@@ -190,36 +190,20 @@
     final = UNITS - PAIR
     ready(final, PAIR)
     tokens = tokens_ref[...] - me * local_vocab
-    blocks = local_vocab // rows
-    inner = 3 if blocks % 3 == 0 else 1
-
-    big = rows * inner
-
-    def measure(i, carry):
-        top, total, picked = carry
-        for b in range(inner):
-            low = pl.multiple_of(i * big + b * rows, 8)
-            logits = acc[pl.ds(low, rows), :]
-            new_top = jnp.maximum(top, jnp.max(logits, axis=0, keepdims=True))
-            line = lax.broadcasted_iota(jnp.int32, logits.shape, 0)
-            picked += jnp.sum(jnp.where(line == tokens - low, logits, 0.0), axis=0, keepdims=True)
-            total = total * jnp.exp(top - new_top) + jnp.sum(jnp.exp(logits - new_top), axis=0, keepdims=True)
-            top = new_top
-        return top, total, picked
-
-    def finalize(i):
-        low = pl.multiple_of(i * big, 8)
-        acc[pl.ds(low, big), :] += product(final, low, big, PAIR * unit)
-
-    def close(i, carry):
-        carry = measure(i - 1, carry)
-        finalize(i)
-        return carry
-
-    carry = (jnp.full((1, seqs), -jnp.inf, jnp.float32),) + (jnp.zeros((1, seqs), jnp.float32),) * 2
-    finalize(0)
-    carry = lax.fori_loop(1, blocks // inner, close, carry)
-    top, total, picked = measure(blocks // inner - 1, carry)
+    top = jnp.full((1, seqs), -jnp.inf, jnp.float32)
+    picked = jnp.zeros((1, seqs), jnp.float32)
+    for low in range(0, local_vocab, rows):
+        logits = acc[low:low + rows, :] + product(final, low, rows, PAIR * unit)
+        acc[low:low + rows, :] = logits
+        line = lax.broadcasted_iota(jnp.int32, logits.shape, 0)
+        picked += jnp.sum(jnp.where(line == tokens - low, logits, 0.0), axis=0, keepdims=True)
+        top = jnp.maximum(top, jnp.max(logits, axis=0, keepdims=True))
+
+    def add(i, total):
+        part = acc[pl.ds(pl.multiple_of(i * rows, 8), rows), :]
+        return total + jnp.sum(jnp.exp(part - top), axis=0, keepdims=True)
+
+    total = lax.fori_loop(0, local_vocab // rows, add, jnp.zeros((1, seqs), jnp.float32))
 
     groups, _, _, lanes = sent.shape
     for g in range(groups):
@@ -272,11 +256,11 @@
     per_device, depth = hidden.shape
     local_vocab = head.shape[0]
     seqs = per_device * devices
-    rows = chunk_rows(local_vocab, 528)
+    rows = chunk_rows(local_vocab, 1584)
     unit = depth // UNITS
     fixed = local_vocab * seqs * 4 + 2 * seqs * depth * 2 + 3 * 2**20
     wide = PAIR * unit
-    slots = min(depth // wide, (VMEM - fixed - local_vocab * seqs * 5) // (local_vocab * wide * 2))
+    slots = min(3, depth // wide, (VMEM - fixed - local_vocab * seqs * 5) // (local_vocab * wide * 2))
     stores = [tuple(dims[a] for a in reversed(path)) for path in ((0, 1, 2, 3), (0, 2, 1, 3))]
     lanes = 128
     out = pl.pallas_call(

time: 56 us -> 54.2 us (0.968)
  Pallas kernels: 54.4 us -> 52.7 us
    pallas_call x1, Pallas kernels: 54.4 us -> 52.7 us  [shards(): pl.pallas_call(functools.partial(kernel, dims, unit, rows), out_shape=jax...]
where the time goes in v2:
time: 54.2 us; the launch traced here: 54 us
  Pallas kernels  52.7 us (97%)
  local copies, waits for them, and re-layouts  1.31 us (2%)
    pallas_call x1, Pallas kernels, shards(): pl.pallas_call(functools.partial(kernel, dims, unit, rows), out_shape=jax...  52.7 us
    slice x1, local copies, waits for them, and re-layouts, shards(): return out[:, 0]  1.31 us

profile of v2, /device:TPU:0, one launch (start us, length us, event | category | flops | bytes accessed | tf_op | source)
XLA Modules:
  0.0 54.0 jit_solution(6138543161028507816)
XLA Ops:
  0.0 52.7 %shard_map.37 = f32[8,128]{1,0:T(8,128)} custom-call(s32[1,256]{1,0:T(1,128)} %bitcast.1, bf16[8,8192]{1,0:T(8,128)(2,1)} %hidden_ref.1, bf16[4752,8192]{1,0:T(8,128)(2,1)} %head_ref.1), custom_call_target="tpu_custom_call" | custom-call | tf_op jit(solution)/shard_map/pallas_call | solution.py:266
  52.7 1.3 %slice_reduce_fusion = f32[8]{0:T(128)} fusion(f32[8,128]{1,0:T(8,128)} %shard_map.37), kind=kLoop, calls=%fused_computation | loop fusion | bytes 64 | tf_op jit(solution)/shard_map/slice | solution.py:290
